TPU v7x, 32 devices: a whole 2x2x4 slice. The times are simulated.
32 devices in a mesh: groups: 2 (over y), blk: 16 (over z, x, core).
Axes of the slice: x: 2, y: 2, z: 4, core: 2. Of those that a mesh axis runs over, the one named last changes fastest.
Arguments:
- current_states: float32 [16, 8192], P(None, ('groups', 'blk')), parts along dimension 1, may hold values from -0.5 to 0.5
- next_states: float32 [16, 8192], P(None, ('groups', 'blk')), parts along dimension 1, may hold values from -1 to 1
- next_values: float32 [8192], P(('groups', 'blk')), parts along dimension 0, may hold values from 0 to 2.5
- vol_table: float32 [12, 16], replicated, may hold values from 0.15 to 0.45
- date_index: int32 [1], replicated, may hold values from 0 to 11
- strike: float32 [1], replicated, may hold values from 0.8 to 1.2
Outputs:
- continuation: float32 [8192], P(('groups', 'blk')), parts along dimension 0
- node_value: float32 [8192], P(('groups', 'blk')), parts along dimension 0
There are 2 independent parts, one for each index of `groups`. A program takes and returns all parts, laid end to end along the dimension named above; an argument that names none is the same for every part. Nothing has to cross between parts.
All inputs are finite; a program needn't handle non-finite values.
Results may differ from a plain program's by a relative error of at most 0.00012.
Values sent between devices are 32-bit elements; how exact they have to be, the bound alone decides.
A program may use at most 64 MiB of HBM per device.

v0:
```python
import math

import jax
import jax.numpy as jnp
from jax import lax
from jax.sharding import PartitionSpec as P

rate_year = 0.05
step_years = 0.1


def scaled_states(current_states, next_states, vol_table, date_index):
    date_count = vol_table.shape[0]
    picked = (jnp.arange(date_count, dtype=jnp.int32) == date_index[0]).astype(jnp.float32)
    vol_row = jnp.sum(vol_table * picked[:, None], axis=0)
    spread = vol_row * math.sqrt(step_years)
    drift_term = (rate_year - 0.5 * vol_row * vol_row) * step_years
    anchor = (current_states + drift_term[:, None]) / spread[:, None]
    target = next_states / spread[:, None]
    anchor_half = 0.5 * jnp.sum(anchor * anchor, axis=0, keepdims=True)
    target_half = 0.5 * jnp.sum(target * target, axis=0, keepdims=True)
    return (anchor, anchor_half, target, target_half)


def kernel_block(source_states, source_norms, sink_states, sink_norms):
    inner_term = lax.dot_general(
        source_states,
        sink_states,
        (((0,), (0,)), ((), ())),
        precision=lax.Precision.HIGHEST,
        preferred_element_type=jnp.float32,
    )
    return jnp.exp(inner_term - source_norms.reshape(-1, 1) - sink_norms)


def block_rows(row_count):
    if row_count <= 4096:
        return row_count
    return math.gcd(row_count, 4096)


def finish(current_states, totals, strike):
    continuation = math.exp(-rate_year * step_years) * totals[0] / totals[1]
    payoff = jnp.maximum(jnp.max(jnp.exp(current_states), axis=0) - strike[0], 0.0)
    return (continuation, jnp.maximum(payoff, continuation))


def body(current_states, next_states, next_values, vol_table, date_index, strike):
    anchor, anchor_half, target, target_half = scaled_states(
        current_states, next_states, vol_table, date_index
    )
    local_count = anchor.shape[1]
    pieces = (
        lax.all_gather(anchor, "blk", axis=1, tiled=True),
        lax.all_gather(anchor_half, "blk", axis=1, tiled=True),
    )
    row_count = pieces[0].shape[1]
    block_size = block_rows(row_count)

    def one_block(number, inner_sum):
        source_part = lax.dynamic_slice_in_dim(pieces[0], number * block_size, block_size, 1)
        norm_part = lax.dynamic_slice_in_dim(pieces[1], number * block_size, block_size, 1)
        return inner_sum + jnp.sum(
            kernel_block(source_part, norm_part, target, target_half), axis=0
        )

    density = lax.fori_loop(
        0, row_count // block_size, one_block, jnp.zeros((local_count,), jnp.float32)
    )
    extras = jnp.concatenate(
        [target_half, (next_values / density)[None, :], (1.0 / density)[None, :]], axis=0
    )
    add_pieces = (
        lax.all_gather(target, "blk", axis=1, tiled=True),
        lax.all_gather(extras, "blk", axis=1, tiled=True),
    )
    row_count = add_pieces[0].shape[1]
    add_block_size = block_rows(row_count)

    def one_block(number, inner_sum):
        sink_part = lax.dynamic_slice_in_dim(
            add_pieces[0], number * add_block_size, add_block_size, 1
        )
        extra_part = lax.dynamic_slice_in_dim(
            add_pieces[1], number * add_block_size, add_block_size, 1
        )
        weights = kernel_block(sink_part, extra_part[0:1], anchor, anchor_half)
        return inner_sum + jnp.dot(
            extra_part[1:3],
            weights,
            precision=lax.Precision.HIGHEST,
            preferred_element_type=jnp.float32,
        )

    totals = lax.fori_loop(
        0, row_count // add_block_size, one_block, jnp.zeros((2, local_count), jnp.float32)
    )
    return finish(current_states, totals, strike)


def solution(mesh):
    placed = (
        P(None, ("groups", "blk")),
        P(None, ("groups", "blk")),
        P(("groups", "blk")),
        P(),
        P(),
        P(),
    )
    return jax.shard_map(
        body,
        mesh=mesh,
        in_specs=placed,
        out_specs=(P(("groups", "blk")), P(("groups", "blk"))),
        check_vma=False,
    )
```

profile of v0, /device:TPU:0, one launch (start us, length us, event | category | flops | bytes accessed | tf_op | source)
XLA Modules:
  0.0 93.4 jit_solution(17060757897564297539)
XLA Ops:
  0.6 0.0 copy-start.1
  1.3 0.8 multiply_reduce_fusion.2
  2.1 0.8 multiply_reduce_fusion
  2.9 23.8 %all_gather.12 = f32[16,4096]{1,0:T(8,128)S(1)} all-gather(f32[16,256]{1,0:T(8,128)S(1)} %get-tuple-element.33), channel_id=1, replica_groups=mesh['groups'=2,'blk'=16] {'blk'}, dimensions={1}, use_global_device_ids=true | all-gather | bytes 278528 | tf_op jit(solution)/shard_map/all_gather | solution.py:54
  26.7 17.5 %all-gather.1 = f32[16,1,256]{2,1,0:T(1,128)S(1)} all-gather(f32[1,1,256]{2,1,0:T(1,128)S(1)} %bitcast.18), channel_id=2, replica_groups=mesh['groups'=2,'blk'=16] {'blk'}, dimensions={0}, use_global_device_ids=true | all-gather | bytes 17408 | tf_op jit(solution)/shard_map/all_gather | solution.py:55
  44.2 4.4 %fusion.4 = f32[256]{0:T(256)S(1)} fusion(f32[256]{0:T(256)S(1)} %broadcast_multiply_fusion.1, f32[4096]{0:T(1024)S(1)} %bitcast.17, f32[16,4096]{1,0:T(8,128)S(1)} %all_gather.12, f32[16,256]{1,0:T(8,128)S(1)} %get-tuple-element.45), kind=kOutput, calls=%fused_computation.6 | convolution fusion | flops 204472064 | bytes 296960 | tf_op jit(solution)/shard_map/while/body/eval_jaxpr/dot_general | solution.py:26
  48.6 0.0 copy-done.1
  48.7 18.9 %all_gather.14 = f32[3,4096]{1,0:T(4,128)S(1)} all-gather(f32[3,256]{1,0:T(4,128)S(1)} %pad_maximum_fusion), channel_id=1, replica_groups=mesh['groups'=2,'blk'=16] {'blk'}, dimensions={1}, use_global_device_ids=true | all-gather | bytes 52224 | tf_op jit(solution)/shard_map/all_gather | solution.py:75
  67.6 18.2 %all_gather.15 = f32[16,4096]{1,0:T(8,128)S(1)} all-gather(f32[16,256]{1,0:T(8,128)S(1)} %get-tuple-element.45), channel_id=1, replica_groups=mesh['groups'=2,'blk'=16] {'blk'}, dimensions={1}, use_global_device_ids=true | all-gather | bytes 278528 | tf_op jit(solution)/shard_map/all_gather | solution.py:74
  85.8 4.6 %fusion.1 = f32[4096,256]{1,0:T(8,128)S(1)} fusion(f32[16,4096]{1,0:T(8,128)S(1)} %all_gather.15, f32[16,256]{1,0:T(8,128)S(1)} %get-tuple-element.33, f32[256]{0:T(256)S(1)} %broadcast_multiply_fusion, f32[4096]{0:T(1024)S(1)} %bitcast.16), kind=kOutput, calls=%fused_computation.2 | convolution fusion | flops 203423744 | bytes 4490240 | tf_op jit(solution)/shard_map/while/body/eval_jaxpr/dot_general | solution.py:26
  90.4 1.7 %fusion.5 = f32[2,256]{1,0:T(2,128)S(1)} fusion(f32[4096,256]{1,0:T(8,128)S(1)} %fusion.1, f32[3,4096]{1,0:T(4,128)S(1)} %all_gather.14), kind=kOutput, calls=%fused_computation.7 | convolution fusion | flops 25165824 | bytes 4229120 | tf_op jit(solution)/shard_map/while/body/eval_jaxpr/dot_general | solution.py:88
  92.2 0.0 copy-start
  92.8 0.6 maximum_maximum_fusion
  93.4 0.0 copy-done
  (8 shorter events, 0.1 us)
Async XLA Ops:
  0.6 48.0 %copy-start.1 = (f32[256]{0:T(256)S(1)}, f32[256]{0:T(256)}, u32[]{:S(2)}) copy-start(f32[256]{0:T(256)} %param.8) | copy-start | bytes 3076
  92.2 1.2 %copy-start = (f32[1,256]{1,0:T(1,128)}, f32[1,256]{1,0:T(1,128)S(1)}, u32[]{:S(2)}) copy-start(f32[1,256]{1,0:T(1,128)S(1)} %slice_divide_fusion) | copy-start | bytes 3076
where the time goes:
time: 93.8 us; the launch traced here: 93.4 us
  blocking collectives  78.4 us (84%)
  matrix products  10.8 us (12%)
  other arithmetic  2.22 us (2%)
  between operations  2.02 us (2%)
    all_gather x1, blocking collectives, body(): lax.all_gather(anchor, 'blk', axis=1, tiled=True)  23.8 us
    all_gather x1, blocking collectives, body(): lax.all_gather(extras, 'blk', axis=1, tiled=True)  18.9 us
    all_gather x1, blocking collectives, body(): lax.all_gather(target, 'blk', axis=1, tiled=True)  18.2 us
    all_gather x1, blocking collectives, body(): lax.all_gather(anchor_half, 'blk', axis=1, tiled=True)  17.5 us
    dot_general x2, matrix products, kernel_block(): lax.dot_general(source_states, sink_states, (((0,), (0,)), ((), ())), pre...  9.04 us

commit v1 on v0

v1 whole, which is shorter than its diff:
```python
import functools
import math

import jax
import jax.numpy as jnp
from jax import lax
from jax.experimental import pallas as pl
from jax.experimental.pallas import tpu as pltpu
from jax.sharding import PartitionSpec as P

rate_year = 0.05
step_years = 0.1
MESH = pl.DeviceIdType.MESH


def inner_size(count):
    size = 1
    while count % (2 * size) == 0 and (2 * size) ** 2 <= count:
        size *= 2
    return size


def split3(x):
    high = x.astype(jnp.bfloat16)
    rest = x - high.astype(jnp.float32)
    mid = rest.astype(jnp.bfloat16)
    low = (rest - mid.astype(jnp.float32)).astype(jnp.bfloat16)
    return high, mid, low


def norm_rows(x, first):
    norm = -0.5 * jnp.sum(x * x, axis=0, keepdims=True)
    pieces = [piece.astype(jnp.float32) for piece in split3(norm)]
    row = lax.broadcasted_iota(jnp.int32, (16, x.shape[1]), 0)
    at = 0 if first else 3
    rows = jnp.where((row >= 3 - at) & (row < 6 - at), 1.0, 0.0)
    for number, piece in enumerate(pieces):
        rows = jnp.where(row == at + number, piece, rows)
    return rows.astype(jnp.bfloat16)


def anchor_stack(x):
    high, mid, low = split3(x)
    zero = jnp.zeros_like(high)
    return jnp.concatenate([high, high, high, mid, mid, low, norm_rows(x, True), zero], axis=0)


def target_stack(x):
    high, mid, low = split3(x)
    zero = jnp.zeros_like(high)
    return jnp.concatenate([high, mid, low, high, mid, high, norm_rows(x, False), zero], axis=0)


def kernel(
    inner_count,
    outer_count,
    cur_hbm,
    next_hbm,
    val_hbm,
    vol_hbm,
    date_hbm,
    strike_hbm,
    out_ref,
    anc,
    tgt,
    val,
    vol,
    date,
    strike,
    kmat,
    tstack,
    dens_own,
    dens_in,
    part_own,
    part_in,
    in_sem,
    anc_send,
    anc_recv,
    tgt_send,
    tgt_recv,
    val_send,
    val_recv,
    dens_send,
    dens_recv,
    part_send,
    part_recv,
):
    g, h = inner_count, outer_count
    n = anc.shape[2]
    me = lax.axis_index("blk")
    inner, outer = lax.rem(me, g), lax.div(me, g)

    def inner_peer(s):
        return {"blk": outer * g + lax.rem(inner + s, g)}

    def outer_peer(s):
        return {"blk": lax.rem(outer + s, h) * g + inner}

    barrier = pltpu.get_barrier_semaphore()
    for s in range(1, h):
        pl.semaphore_signal(barrier, inc=1, device_id=outer_peer(s), device_id_type=MESH)
    for s in range(1, g):
        pl.semaphore_signal(barrier, inc=1, device_id=inner_peer(s), device_id_type=MESH)

    loads = [
        pltpu.make_async_copy(src, dst, in_sem.at[number])
        for number, (src, dst) in enumerate(
            [
                (cur_hbm, anc.at[0]),
                (next_hbm, tgt.at[inner]),
                (val_hbm, val.at[inner]),
                (vol_hbm, vol),
                (date_hbm, date),
                (strike_hbm, strike),
            ]
        )
    ]
    for load in loads:
        load.start()
    for load in loads:
        load.wait()

    dates, assets = vol.shape
    picked = lax.broadcasted_iota(jnp.int32, (dates, assets), 0) == date[0]
    vol_lanes = jnp.sum(jnp.where(picked, vol[...], 0.0), axis=0, keepdims=True)
    eye = lax.broadcasted_iota(jnp.int32, (assets, assets), 0) == lax.broadcasted_iota(
        jnp.int32, (assets, assets), 1
    )
    vol_row = jnp.sum(jnp.where(eye, vol_lanes, 0.0), axis=1, keepdims=True)
    scale = math.sqrt(math.log2(math.e)) / (vol_row * math.sqrt(step_years))
    drift = (rate_year - 0.5 * vol_row * vol_row) * step_years

    pl.semaphore_wait(barrier, (h - 1) + (g - 1))

    anc_copies, tgt_copies, val_copies = {}, {}, {}
    far_first = sorted(range(1, h), key=lambda s: -min(s, h - s))
    for s in far_first:
        anc_copies[s] = pltpu.make_async_remote_copy(
            src_ref=anc.at[0],
            dst_ref=anc.at[s],
            send_sem=anc_send.at[s],
            recv_sem=anc_recv.at[s],
            device_id=outer_peer(s),
            device_id_type=MESH,
        )
        anc_copies[s].start()
    for s in range(1, g):
        tgt_copies[s] = pltpu.make_async_remote_copy(
            src_ref=tgt.at[inner],
            dst_ref=tgt.at[inner],
            send_sem=tgt_send.at[s],
            recv_sem=tgt_recv.at[s],
            device_id=inner_peer(s),
            device_id_type=MESH,
        )
        tgt_copies[s].start()
    for s in range(1, g):
        val_copies[s] = pltpu.make_async_remote_copy(
            src_ref=val.at[inner],
            dst_ref=val.at[inner],
            send_sem=val_send.at[s],
            recv_sem=val_recv.at[s],
            device_id=inner_peer(s),
            device_id_type=MESH,
        )
        val_copies[s].start()

    def anchor_rows(s):
        stack = anchor_stack((anc[s] + drift) * scale)
        return jnp.transpose(stack)

    own_rows = anchor_rows(0)
    for s in range(1, g):
        tgt_copies[s].wait_recv()
    for q in range(g):
        tstack[:, q * n : (q + 1) * n] = target_stack(tgt[q] * scale)

    density = jnp.zeros((8, g * n), jnp.float32)
    for s in [0] + far_first[::-1]:
        if s:
            anc_copies[s].wait_recv()
            rows = anchor_rows(s)
        else:
            rows = own_rows
        exponent = jnp.dot(rows, tstack[...], preferred_element_type=jnp.float32)
        block = jnp.exp2(exponent)
        kmat[s] = block
        density = density + jnp.sum(block.reshape(n // 8, 8, g * n), axis=0)

    dens_own[...] = jnp.sum(density, axis=0, keepdims=True)
    dens_copies = {}
    for s in range(1, g):
        dens_copies[s] = pltpu.make_async_remote_copy(
            src_ref=dens_own,
            dst_ref=dens_in.at[s],
            send_sem=dens_send.at[s],
            recv_sem=dens_recv.at[s],
            device_id=inner_peer(s),
            device_id_type=MESH,
        )
        dens_copies[s].start()
    payoff = jnp.maximum(
        jnp.max(jnp.exp(anc[0]), axis=0, keepdims=True) - strike[0], 0.0
    )
    for s in range(1, g):
        val_copies[s].wait_recv()
    total = dens_own[...]
    for s in range(1, g):
        dens_copies[s].wait_recv()
        total = total + dens_in[s]
    inverse = 1.0 / total
    values = jnp.concatenate([val[q] for q in range(g)], axis=1)
    worth = values / total

    part_copies = {}
    for s in far_first + [0]:
        weighted = jnp.zeros((n, 128), jnp.float32)
        mass = jnp.zeros((n, 128), jnp.float32)
        for q in range(g * n // 128):
            tile = kmat[s, :, q * 128 : (q + 1) * 128]
            weighted = weighted + tile * worth[:, q * 128 : (q + 1) * 128]
            mass = mass + tile * inverse[:, q * 128 : (q + 1) * 128]
        part_own[s, 0:1, :] = jnp.sum(jnp.transpose(weighted), axis=0, keepdims=True)
        part_own[s, 1:2, :] = jnp.sum(jnp.transpose(mass), axis=0, keepdims=True)
        if s:
            part_copies[s] = pltpu.make_async_remote_copy(
                src_ref=part_own.at[s],
                dst_ref=part_in.at[s],
                send_sem=part_send.at[s],
                recv_sem=part_recv.at[s],
                device_id=outer_peer(h - s),
                device_id_type=MESH,
            )
            part_copies[s].start()
    sums = part_own[0]
    for s in far_first[::-1]:
        part_copies[s].wait_recv()
        sums = sums + part_in[s]
    out_ref[0:2, :] = sums
    out_ref[2:3, :] = payoff
    for copies in (anc_copies, tgt_copies, val_copies, dens_copies, part_copies):
        for copy in copies.values():
            copy.wait_send()


def body(count, current_states, next_states, next_values, vol_table, date_index, strike):
    assets, n = current_states.shape
    g = inner_size(count)
    h = count // g
    f32 = jnp.float32
    dma = pltpu.SemaphoreType.DMA
    sums = pl.pallas_call(
        functools.partial(kernel, g, h),
        out_shape=jax.ShapeDtypeStruct((3, n), f32),
        in_specs=[pl.BlockSpec(memory_space=pl.ANY)] * 6,
        out_specs=pl.BlockSpec(memory_space=pltpu.VMEM),
        scratch_shapes=[
            pltpu.VMEM((h, assets, n), f32),
            pltpu.VMEM((g, assets, n), f32),
            pltpu.VMEM((g, 1, n), f32),
            pltpu.VMEM(vol_table.shape, f32),
            pltpu.SMEM((1,), jnp.int32),
            pltpu.SMEM((1,), f32),
            pltpu.VMEM((h, n, g * n), f32),
            pltpu.VMEM((128, g * n), jnp.bfloat16),
            pltpu.VMEM((1, g * n), f32),
            pltpu.VMEM((g, 1, g * n), f32),
            pltpu.VMEM((h, 2, n), f32),
            pltpu.VMEM((h, 2, n), f32),
            dma((6,)),
            dma((h,)),
            dma((h,)),
            dma((g,)),
            dma((g,)),
            dma((g,)),
            dma((g,)),
            dma((g,)),
            dma((g,)),
            dma((h,)),
            dma((h,)),
        ],
        compiler_params=pltpu.CompilerParams(collective_id=0, has_side_effects=True),
    )(current_states, next_states, next_values.reshape(1, n), vol_table, date_index, strike)
    continuation = math.exp(-rate_year * step_years) * sums[0] / sums[1]
    return (continuation, jnp.maximum(sums[2], continuation))


def solution(mesh):
    placed = (
        P(None, ("groups", "blk")),
        P(None, ("groups", "blk")),
        P(("groups", "blk")),
        P(),
        P(),
        P(),
    )
    return jax.shard_map(
        functools.partial(body, mesh.shape["blk"]),
        mesh=mesh,
        in_specs=placed,
        out_specs=(P(("groups", "blk")), P(("groups", "blk"))),
        check_vma=False,
    )
```

time: 93.8 us -> 22.4 us (0.24)
  blocking collectives: 78.4 us -> 0 us
  Pallas kernels: 0 us -> 18.2 us
  matrix products: 10.8 us -> 0 us
    all_gather x4 -> x0, blocking collectives: 78.4 us -> none  [the longest x1 23.8 us: body(): lax.all_gather(anchor, 'blk', axis=1, tiled=True)]
    pallas_call x0 -> x1, Pallas kernels: none -> 18.2 us  [body(): pl.pallas_call(functools.partial(kernel, g, h), out_shape=jax.ShapeDtypeS...]
    dot_general x3 -> x0, matrix products: 10.8 us -> none  [the longest x2 9.04 us: kernel_block(): lax.dot_general(source_states, sink_states, (((0,), (0,)), ((), ())), pre...]
    reduce_sum x2 -> x0, other arithmetic: 1.61 us -> none  [the longest x1 0.82 us: scaled_states(): anchor_half = 0.5 * jnp.sum(anchor * anchor, axis=0, keepdims=True)]
where the time goes in v1:
time: 22.4 us; the launch traced here: 22.1 us
  Pallas kernels  18.2 us (81%)
  between operations  1.93 us (9%)
  other arithmetic  1.35 us (6%)
  local copies, waits for them, and re-layouts  0.56 us (3%)
    pallas_call x1, Pallas kernels, body(): pl.pallas_call(functools.partial(kernel, g, h), out_shape=jax.ShapeDtypeS...  18.2 us
    slice x1, other arithmetic, body(): return (continuation, jnp.maximum(sums[2], continuation))  0.79 us
    max x1, other arithmetic, body(): return (continuation, jnp.maximum(sums[2], continuation))  0.56 us
    unnamed x2, local copies, waits for them, and re-layouts  0.56 us

profile of v1, /device:TPU:0, one launch (start us, length us, event | category | flops | bytes accessed | tf_op | source)
XLA Modules:
  0.0 22.1 jit_solution(15581481654553221569)
XLA Ops:
  1.9 18.2 %shard_map.77 = f32[3,256]{1,0:T(4,128)} custom-call(f32[16,256]{1,0:T(8,128)} %cur_hbm.1, f32[16,256]{1,0:T(8,128)} %next_hbm.1, f32[1,256]{1,0:T(1,128)} %bitcast.6, f32[12,16]{1,0:T(8,128)} %vol_hbm.1, s32[1]{0:T(128)S(6)} %copy.8.date_hbm, f32[1]{0:T(128)S(6)} %copy.9.strike_hbm), custom_call_target="tpu_custom_call" | custom-call | tf_op jit(solution)/shard_map/pallas_call | solution.py:252
  20.2 0.8 %fusion = (f32[1,256]{1,0:T(1,128)S(1)}, f32[1,256]{1,0:T(1,128)S(1)}) fusion(f32[3,256]{1,0:T(4,128)} %shard_map.77), kind=kLoop, calls=%fused_computation.1 | loop fusion | flops 512 | bytes 5120 | tf_op jit(solution)/shard_map/slice | solution.py:285
  21.0 0.0 copy-start
  21.0 0.6 %copy-done = f32[1,256]{1,0:T(1,128)} copy-done((f32[1,256]{1,0:T(1,128)}, f32[1,256]{1,0:T(1,128)S(1)}, u32[]{:S(2)}) %copy-start) | copy-done | bytes 1048
  21.5 0.6 %max.3 = f32[256]{0:T(256)} maximum(f32[256]{0:T(256)S(1)} %bitcast.5, f32[256]{0:T(256)S(1)} %bitcast.3) | non-fusion elementwise | flops 256 | bytes 3072 | tf_op jit(solution)/shard_map/max | solution.py:285
Async XLA Ops:
  21.0 0.6 %copy-start = (f32[1,256]{1,0:T(1,128)}, f32[1,256]{1,0:T(1,128)S(1)}, u32[]{:S(2)}) copy-start(f32[1,256]{1,0:T(1,128)S(1)} %get-tuple-element.3) | copy-start | bytes 3076

commit v2 on v1

v2 whole, which is shorter than its diff:
```python
import functools
import math

import jax
import jax.numpy as jnp
from jax import lax
from jax.experimental import pallas as pl
from jax.experimental.pallas import tpu as pltpu
from jax.sharding import PartitionSpec as P

rate_year = 0.05
step_years = 0.1
MESH = pl.DeviceIdType.MESH


def inner_size(count):
    size = 1
    while count % (2 * size) == 0 and (2 * size) ** 2 <= count:
        size *= 2
    return size


def radices(size):
    digits = size.bit_length() - 1
    return (2,) * digits if 2**digits == size else (size,)


def moved(place, offset, size, sign):
    result, unit = 0, 1
    for radix in radices(size):
        digit = (place // unit + sign * (offset // unit % radix) + radix) % radix
        result = result + digit * unit
        unit *= radix
    return result


def digit_count(offset):
    return bin(offset).count("1")


def split3(x):
    high = x.astype(jnp.bfloat16)
    rest = x - high.astype(jnp.float32)
    mid = rest.astype(jnp.bfloat16)
    low = (rest - mid.astype(jnp.float32)).astype(jnp.bfloat16)
    return high, mid, low


def norm_rows(x, first):
    norm = -0.5 * jnp.sum(x * x, axis=0, keepdims=True)
    pieces = [piece.astype(jnp.float32) for piece in split3(norm)]
    row = lax.broadcasted_iota(jnp.int32, (16, x.shape[1]), 0)
    at = 0 if first else 3
    rows = jnp.where((row >= 3 - at) & (row < 6 - at), 1.0, 0.0)
    for number, piece in enumerate(pieces):
        rows = jnp.where(row == at + number, piece, rows)
    return rows.astype(jnp.bfloat16)


def anchor_stack(x):
    high, mid, low = split3(x)
    zero = jnp.zeros_like(high)
    return jnp.concatenate([high, high, high, mid, mid, low, norm_rows(x, True), zero], axis=0)


def target_stack(x):
    high, mid, low = split3(x)
    zero = jnp.zeros_like(high)
    return jnp.concatenate([high, mid, low, high, mid, high, norm_rows(x, False), zero], axis=0)


def kernel(
    inner_count,
    outer_count,
    cur_hbm,
    next_hbm,
    val_hbm,
    vol_hbm,
    date_hbm,
    strike_hbm,
    cont_ref,
    node_ref,
    anc,
    tgt,
    val,
    vol,
    date,
    strike,
    kmat,
    dens_own,
    dens_in,
    part_own,
    part_in,
    in_sem,
    anc_send,
    anc_recv,
    tgt_send,
    tgt_recv,
    val_send,
    val_recv,
    dens_send,
    dens_recv,
    part_send,
    part_recv,
):
    g, h = inner_count, outer_count
    n = anc.shape[2]
    low_count = min(g, 2)
    me = lax.axis_index("blk")
    low = me % low_count
    outer = me // low_count % h
    inner = me // (low_count * h) * low_count + low

    def place(inner_place, outer_place):
        high = inner_place // low_count
        return {"blk": (high * h + outer_place) * low_count + inner_place % low_count}

    def inner_peer(q):
        return place(moved(inner, q, g, 1), outer)

    def outer_peer(s, sign=1):
        return place(inner, moved(outer, s, h, sign))

    def owner(q):
        return moved(inner, q, g, -1)

    inner_offsets = list(range(g - 1, 0, -1))
    outer_offsets = sorted(range(1, h), key=lambda s: (-digit_count(s), -s))

    barrier = pltpu.get_barrier_semaphore()
    for q in inner_offsets:
        pl.semaphore_signal(barrier, inc=1, device_id=inner_peer(q), device_id_type=MESH)
    for s in outer_offsets:
        pl.semaphore_signal(barrier, inc=1, device_id=outer_peer(s), device_id_type=MESH)

    loads = [
        pltpu.make_async_copy(src, dst, in_sem.at[number])
        for number, (src, dst) in enumerate(
            [
                (next_hbm, tgt.at[inner]),
                (cur_hbm, anc.at[0]),
                (vol_hbm, vol),
                (date_hbm, date),
                (val_hbm, val.at[inner]),
                (strike_hbm, strike),
            ]
        )
    ]
    for load in loads:
        load.start()

    def inner_copies(ref, dst, send, recv):
        return {
            q: pltpu.make_async_remote_copy(
                src_ref=ref,
                dst_ref=dst(q),
                send_sem=send.at[q],
                recv_sem=recv.at[q],
                device_id=inner_peer(q),
                device_id_type=MESH,
            )
            for q in inner_offsets
        }

    tgt_copies = inner_copies(tgt.at[inner], lambda q: tgt.at[inner], tgt_send, tgt_recv)
    val_copies = inner_copies(val.at[inner], lambda q: val.at[inner], val_send, val_recv)
    dens_copies = inner_copies(dens_own, lambda q: dens_in.at[q], dens_send, dens_recv)
    anc_copies = {
        s: pltpu.make_async_remote_copy(
            src_ref=anc.at[0],
            dst_ref=anc.at[s],
            send_sem=anc_send.at[s],
            recv_sem=anc_recv.at[s],
            device_id=outer_peer(s),
            device_id_type=MESH,
        )
        for s in outer_offsets
    }
    part_copies = {
        s: pltpu.make_async_remote_copy(
            src_ref=part_own.at[s],
            dst_ref=part_in.at[s],
            send_sem=part_send.at[s],
            recv_sem=part_recv.at[s],
            device_id=outer_peer(s, -1),
            device_id_type=MESH,
        )
        for s in outer_offsets
    }

    pl.semaphore_wait(barrier, (h - 1) + (g - 1))
    loads[0].wait()
    for q in inner_offsets:
        tgt_copies[q].start()
    loads[1].wait()
    for s in outer_offsets:
        anc_copies[s].start()
    for load in loads[2:]:
        load.wait()
    for q in inner_offsets:
        val_copies[q].start()

    dates, assets = vol.shape
    picked = lax.broadcasted_iota(jnp.int32, (dates, assets), 0) == date[0]
    vol_lanes = jnp.sum(jnp.where(picked, vol[...], 0.0), axis=0, keepdims=True)
    eye = lax.broadcasted_iota(jnp.int32, (assets, assets), 0) == lax.broadcasted_iota(
        jnp.int32, (assets, assets), 1
    )
    vol_row = jnp.sum(jnp.where(eye, vol_lanes, 0.0), axis=1, keepdims=True)
    scale = math.sqrt(math.log2(math.e)) / (vol_row * math.sqrt(step_years))
    drift = (rate_year - 0.5 * vol_row * vol_row) * step_years

    rows, columns = {}, {}
    outer_order = [0] + outer_offsets[::-1]
    near = [q for q in range(g) if q < low_count]
    far = [q for q in range(g) if q >= low_count]

    def block(s, q):
        exponent = jnp.dot(rows[s], columns[q], preferred_element_type=jnp.float32)
        weights = jnp.exp2(exponent)
        kmat[s, :, q * n : (q + 1) * n] = weights
        return jnp.sum(weights.reshape(n // 8, 8, n), axis=0)

    density = {q: jnp.zeros((8, n), jnp.float32) for q in range(g)}
    for part in (near, far):
        for q in part:
            if q:
                tgt_copies[q].wait_recv()
            columns[q] = target_stack(tgt[owner(q)] * scale)
        for s in outer_order:
            if s not in rows:
                if s:
                    anc_copies[s].wait_recv()
                rows[s] = jnp.transpose(anchor_stack((anc[s] + drift) * scale))
            for q in part:
                density[q] = density[q] + block(s, q)
        for q in part:
            dens_own[owner(q)] = jnp.sum(density[q], axis=0, keepdims=True)

    for q in inner_offsets:
        dens_copies[q].start()
    payoff = jnp.maximum(
        jnp.max(jnp.exp(anc[0]), axis=0, keepdims=True) - strike[0], 0.0
    )
    for q in inner_offsets:
        val_copies[q].wait_recv()
    for q in inner_offsets:
        dens_copies[q].wait_recv()
    worth, inverse = {}, {}
    for q in range(g):
        total = dens_own[owner(q)]
        for p in inner_offsets:
            total = total + dens_in[p, owner(q)]
        inverse[q] = 1.0 / total
        worth[q] = val[owner(q)] / total

    for s in outer_order[::-1]:
        weighted = jnp.zeros((n, 128), jnp.float32)
        mass = jnp.zeros((n, 128), jnp.float32)
        for q in range(g):
            for c in range(0, n, 128):
                tile = kmat[s, :, q * n + c : q * n + c + 128]
                weighted = weighted + tile * worth[q][:, c : c + 128]
                mass = mass + tile * inverse[q][:, c : c + 128]
        part_own[s, 0:1, :] = jnp.sum(jnp.transpose(weighted), axis=0, keepdims=True)
        part_own[s, 1:2, :] = jnp.sum(jnp.transpose(mass), axis=0, keepdims=True)
        if s:
            part_copies[s].start()
    sums = part_own[0]
    for s in outer_offsets[::-1]:
        part_copies[s].wait_recv()
        sums = sums + part_in[s]
    continuation = math.exp(-rate_year * step_years) * sums[0:1] / sums[1:2]
    cont_ref[...] = continuation
    node_ref[...] = jnp.maximum(payoff, continuation)
    for copies in (anc_copies, tgt_copies, val_copies, dens_copies, part_copies):
        for copy in copies.values():
            copy.wait_send()


def body(count, current_states, next_states, next_values, vol_table, date_index, strike):
    assets, n = current_states.shape
    g = inner_size(count)
    h = count // g
    f32 = jnp.float32
    dma = pltpu.SemaphoreType.DMA
    row = jax.ShapeDtypeStruct((1, n), f32)
    continuation, node_value = pl.pallas_call(
        functools.partial(kernel, g, h),
        out_shape=(row, row),
        in_specs=[pl.BlockSpec(memory_space=pltpu.HBM)] * 6,
        out_specs=(pl.BlockSpec(memory_space=pltpu.VMEM),) * 2,
        scratch_shapes=[
            pltpu.VMEM((h, assets, n), f32),
            pltpu.VMEM((g, assets, n), f32),
            pltpu.VMEM((g, 1, n), f32),
            pltpu.VMEM(vol_table.shape, f32),
            pltpu.SMEM((1,), jnp.int32),
            pltpu.SMEM((1,), f32),
            pltpu.VMEM((h, n, g * n), f32),
            pltpu.VMEM((g, 1, n), f32),
            pltpu.VMEM((g, g, 1, n), f32),
            pltpu.VMEM((h, 2, n), f32),
            pltpu.VMEM((h, 2, n), f32),
            dma((6,)),
            dma((h,)),
            dma((h,)),
            dma((g,)),
            dma((g,)),
            dma((g,)),
            dma((g,)),
            dma((g,)),
            dma((g,)),
            dma((h,)),
            dma((h,)),
        ],
        compiler_params=pltpu.CompilerParams(collective_id=0, has_side_effects=True),
    )(current_states, next_states, next_values.reshape(1, n), vol_table, date_index, strike)
    return (continuation.reshape(n), node_value.reshape(n))


def solution(mesh):
    placed = (
        P(None, ("groups", "blk")),
        P(None, ("groups", "blk")),
        P(("groups", "blk")),
        P(),
        P(),
        P(),
    )
    return jax.shard_map(
        functools.partial(body, mesh.shape["blk"]),
        mesh=mesh,
        in_specs=placed,
        out_specs=(P(("groups", "blk")), P(("groups", "blk"))),
        check_vma=False,
    )
```

time: 22.4 us -> 20.9 us (0.933)
  other arithmetic: 1.35 us -> 0 us
  Pallas kernels: 18.2 us -> 16.9 us
  local copies, waits for them, and re-layouts: 0.56 us -> 1.86 us
    pallas_call x1, Pallas kernels: 18.2 us -> 16.9 us  [body(): pl.pallas_call(functools.partial(kernel, g, h), out_shape=(row, row), in_...]
    unnamed x2 -> x6, local copies, waits for them, and re-layouts: 0.56 us -> 1.86 us
    slice x1 -> x0, other arithmetic: 0.79 us -> none  [body(): return (continuation, jnp.maximum(sums[2], continuation))]
    max x1 -> x0, other arithmetic: 0.56 us -> none  [body(): return (continuation, jnp.maximum(sums[2], continuation))]
where the time goes in v2:
time: 20.9 us; the launch traced here: 20.6 us
  Pallas kernels  16.9 us (81%)
  between operations  1.94 us (9%)
  local copies, waits for them, and re-layouts  1.86 us (9%)
    pallas_call x1, Pallas kernels, body(): pl.pallas_call(functools.partial(kernel, g, h), out_shape=(row, row), in_...  16.9 us
    unnamed x6, local copies, waits for them, and re-layouts  1.86 us

profile of v2, /device:TPU:0, one launch (start us, length us, event | category | flops | bytes accessed | tf_op | source)
XLA Modules:
  0.0 20.6 jit_solution(7802451731625383321)
XLA Ops:
  1.9 16.9 %shard_map.77 = (f32[1,256]{1,0:T(1,128)}, f32[1,256]{1,0:T(1,128)}) custom-call(f32[16,256]{1,0:T(8,128)} %cur_hbm.1, f32[16,256]{1,0:T(8,128)} %next_hbm.1, f32[1,256]{1,0:T(1,128)} %bitcast.3, f32[12,16]{1,0:T(8,128)} %vol_hbm.1, s32[1]{0:T(128)S(6)} %copy.10.date_hbm, f32[1]{0:T(128)S(6)} %copy.11.strike_hbm), custom_call_target="tpu_custom_call" | custom-call | tf_op jit(solution)/shard_map/pallas_call | solution.py:288
  18.8 0.0 copy-start.1
  18.8 0.7 %copy-done.1 = f32[1,256]{1,0:T(1,128)S(1)} copy-done((f32[1,256]{1,0:T(1,128)S(1)}, f32[1,256]{1,0:T(1,128)}, u32[]{:S(2)}) %copy-start.1) | copy-done | bytes 1048
  19.4 0.0 copy-start
  19.5 0.6 %copy.12 = f32[256]{0:T(256)} copy(f32[256]{0:T(256)S(1)} %bitcast.5) | data formatting | bytes 2048
  20.0 0.1 copy-done
  20.1 0.6 %copy.13 = f32[256]{0:T(256)} copy(f32[256]{0:T(256)S(1)} %bitcast.4) | data formatting | bytes 2048
Async XLA Ops:
  18.8 0.7 %copy-start.1 = (f32[1,256]{1,0:T(1,128)S(1)}, f32[1,256]{1,0:T(1,128)}, u32[]{:S(2)}) copy-start(f32[1,256]{1,0:T(1,128)} %get-tuple-element.4) | copy-start | bytes 3076
  19.4 0.6 %copy-start = (f32[1,256]{1,0:T(1,128)S(1)}, f32[1,256]{1,0:T(1,128)}, u32[]{:S(2)}) copy-start(f32[1,256]{1,0:T(1,128)} %get-tuple-element.5) | copy-start | bytes 3076

commit v3 on v2

--- a/solution.py
+++ b/solution.py
@@ -78,8 +78,9 @@
     vol_hbm,
     date_hbm,
     strike_hbm,
-    cont_ref,
-    node_ref,
+    weighted_ref,
+    mass_ref,
+    payoff_ref,
     anc,
     tgt,
     val,
@@ -270,9 +271,9 @@
     for s in outer_offsets[::-1]:
         part_copies[s].wait_recv()
         sums = sums + part_in[s]
-    continuation = math.exp(-rate_year * step_years) * sums[0:1] / sums[1:2]
-    cont_ref[...] = continuation
-    node_ref[...] = jnp.maximum(payoff, continuation)
+    weighted_ref[...] = sums[0]
+    mass_ref[...] = sums[1]
+    payoff_ref[...] = payoff.reshape(n)
     for copies in (anc_copies, tgt_copies, val_copies, dens_copies, part_copies):
         for copy in copies.values():
             copy.wait_send()
@@ -284,12 +285,12 @@
     h = count // g
     f32 = jnp.float32
     dma = pltpu.SemaphoreType.DMA
-    row = jax.ShapeDtypeStruct((1, n), f32)
-    continuation, node_value = pl.pallas_call(
+    row = pltpu.VMEM((n,), f32)
+    w, m, p = pl.pallas_call(
         functools.partial(kernel, g, h),
-        out_shape=(row, row),
+        out_shape=(row, row, row),
         in_specs=[pl.BlockSpec(memory_space=pltpu.HBM)] * 6,
-        out_specs=(pl.BlockSpec(memory_space=pltpu.VMEM),) * 2,
+        out_specs=(pl.BlockSpec(memory_space=pltpu.VMEM),) * 3,
         scratch_shapes=[
             pltpu.VMEM((h, assets, n), f32),
             pltpu.VMEM((g, assets, n), f32),
@@ -316,7 +317,8 @@
         ],
         compiler_params=pltpu.CompilerParams(collective_id=0, has_side_effects=True),
     )(current_states, next_states, next_values.reshape(1, n), vol_table, date_index, strike)
-    return (continuation.reshape(n), node_value.reshape(n))
+    c = math.exp(-rate_year * step_years) * w / m
+    return (c, jnp.maximum(p, c))
 
 
 def solution(mesh):

time: 20.9 us -> 18.9 us (0.904)
  local copies, waits for them, and re-layouts: 1.86 us -> 0 us
  Pallas kernels: 16.9 us -> 16.3 us
  other arithmetic: 0 us -> 0.58 us
    unnamed x6 -> x0, local copies, waits for them, and re-layouts: 1.86 us -> none
    pallas_call x1, Pallas kernels: 16.9 us -> 16.3 us  [body(): pl.pallas_call(functools.partial(kernel, g, h), out_shape=(row, row, row)...]
    max x0 -> x1, other arithmetic: none -> 0.58 us  [body(): return (c, jnp.maximum(p, c))]
where the time goes in v3:
time: 18.9 us; the launch traced here: 18.8 us
  Pallas kernels  16.3 us (86%)
  between operations  1.93 us (10%)
  other arithmetic  0.58 us (3%)
    pallas_call x1, Pallas kernels, body(): pl.pallas_call(functools.partial(kernel, g, h), out_shape=(row, row, row)...  16.3 us
    max x1, other arithmetic, body(): return (c, jnp.maximum(p, c))  0.58 us

profile of v3, /device:TPU:0, one launch (start us, length us, event | category | flops | bytes accessed | tf_op | source)
XLA Modules:
  0.0 18.8 jit_solution(1037324410396619208)
XLA Ops:
  1.9 16.3 %shard_map.77 = (f32[256]{0:T(256)S(1)}, f32[256]{0:T(256)S(1)}, f32[256]{0:T(256)S(1)}) custom-call(f32[16,256]{1,0:T(8,128)} %cur_hbm.1, f32[16,256]{1,0:T(8,128)} %next_hbm.1, f32[1,256]{1,0:T(1,128)} %bitcast.1, f32[12,16]{1,0:T(8,128)} %vol_hbm.1, s32[1]{0:T(128)S(6)} %copy.8.date_hbm, f32[1]{0:T(128)S(6)} %copy.9.strike_hbm), custom_call_target="tpu_custom_call" | custom-call | tf_op jit(solution)/shard_map/pallas_call | solution.py:289
  18.2 0.6 %fusion = (f32[256]{0:T(256)}, f32[256]{0:T(256)}) fusion(f32[256]{0:T(256)S(1)} %get-tuple-element.7, f32[256]{0:T(256)S(1)} %get-tuple-element.6, f32[256]{0:T(256)S(1)} %get-tuple-element.5), kind=kLoop, calls=%fused_computation.1 | loop fusion | flops 768 | bytes 5120 | tf_op jit(solution)/shard_map/max | solution.py:321

commit v4 on v3

--- a/solution.py
+++ b/solution.py
@@ -77,16 +77,14 @@
     val_hbm,
     vol_hbm,
     date_hbm,
-    strike_hbm,
     weighted_ref,
     mass_ref,
-    payoff_ref,
+    best_ref,
     anc,
     tgt,
     val,
     vol,
     date,
-    strike,
     kmat,
     dens_own,
     dens_in,
@@ -108,13 +106,14 @@
     n = anc.shape[2]
     low_count = min(g, 2)
     me = lax.axis_index("blk")
-    low = me % low_count
     outer = me // low_count % h
+    low = (me + outer * 2 // h) % low_count
     inner = me // (low_count * h) * low_count + low
 
     def place(inner_place, outer_place):
         high = inner_place // low_count
-        return {"blk": (high * h + outer_place) * low_count + inner_place % low_count}
+        turned = (inner_place + outer_place * 2 // h) % low_count
+        return {"blk": (high * h + outer_place) * low_count + turned}
 
     def inner_peer(q):
         return place(moved(inner, q, g, 1), outer)
@@ -143,7 +142,6 @@
                 (vol_hbm, vol),
                 (date_hbm, date),
                 (val_hbm, val.at[inner]),
-                (strike_hbm, strike),
             ]
         )
     ]
@@ -223,7 +221,7 @@
         return jnp.sum(weights.reshape(n // 8, 8, n), axis=0)
 
     density = {q: jnp.zeros((8, n), jnp.float32) for q in range(g)}
-    for part in (near, far):
+    for part in [near] + [[q] for q in reversed(far)]:
         for q in part:
             if q:
                 tgt_copies[q].wait_recv()
@@ -240,9 +238,7 @@
 
     for q in inner_offsets:
         dens_copies[q].start()
-    payoff = jnp.maximum(
-        jnp.max(jnp.exp(anc[0]), axis=0, keepdims=True) - strike[0], 0.0
-    )
+    best = jnp.max(jnp.exp(anc[0]), axis=0, keepdims=True)
     for q in inner_offsets:
         val_copies[q].wait_recv()
     for q in inner_offsets:
@@ -273,7 +269,7 @@
         sums = sums + part_in[s]
     weighted_ref[...] = sums[0]
     mass_ref[...] = sums[1]
-    payoff_ref[...] = payoff.reshape(n)
+    best_ref[...] = best.reshape(n)
     for copies in (anc_copies, tgt_copies, val_copies, dens_copies, part_copies):
         for copy in copies.values():
             copy.wait_send()
@@ -289,7 +285,7 @@
     w, m, p = pl.pallas_call(
         functools.partial(kernel, g, h),
         out_shape=(row, row, row),
-        in_specs=[pl.BlockSpec(memory_space=pltpu.HBM)] * 6,
+        in_specs=[pl.BlockSpec(memory_space=pltpu.HBM)] * 5,
         out_specs=(pl.BlockSpec(memory_space=pltpu.VMEM),) * 3,
         scratch_shapes=[
             pltpu.VMEM((h, assets, n), f32),
@@ -297,13 +293,12 @@
             pltpu.VMEM((g, 1, n), f32),
             pltpu.VMEM(vol_table.shape, f32),
             pltpu.SMEM((1,), jnp.int32),
-            pltpu.SMEM((1,), f32),
             pltpu.VMEM((h, n, g * n), f32),
             pltpu.VMEM((g, 1, n), f32),
             pltpu.VMEM((g, g, 1, n), f32),
             pltpu.VMEM((h, 2, n), f32),
             pltpu.VMEM((h, 2, n), f32),
-            dma((6,)),
+            dma((5,)),
             dma((h,)),
             dma((h,)),
             dma((g,)),
@@ -316,9 +311,9 @@
             dma((h,)),
         ],
         compiler_params=pltpu.CompilerParams(collective_id=0, has_side_effects=True),
-    )(current_states, next_states, next_values.reshape(1, n), vol_table, date_index, strike)
+    )(current_states, next_states, next_values.reshape(1, n), vol_table, date_index)
     c = math.exp(-rate_year * step_years) * w / m
-    return (c, jnp.maximum(p, c))
+    return (c, jnp.maximum(jnp.maximum(p - strike[0], 0.0), c))
 
 
 def solution(mesh):

time: 18.9 us -> 18.6 us (0.984)
  Pallas kernels: 16.3 us -> 15.9 us
    pallas_call x1, Pallas kernels: 16.3 us -> 15.9 us  [body(): pl.pallas_call(functools.partial(kernel, g, h), out_shape=(row, row, row)...]
where the time goes in v4:
time: 18.6 us; the launch traced here: 18.4 us
  Pallas kernels  15.9 us (85%)
  between operations  1.93 us (10%)
  other arithmetic  0.58 us (3%)
    pallas_call x1, Pallas kernels, body(): pl.pallas_call(functools.partial(kernel, g, h), out_shape=(row, row, row)...  15.9 us
    max x1, other arithmetic, body(): return (c, jnp.maximum(jnp.maximum(p - strike[0], 0.0), c))  0.58 us

profile of v4, /device:TPU:0, one launch (start us, length us, event | category | flops | bytes accessed | tf_op | source)
XLA Modules:
  0.0 18.4 jit_solution(16589105285533730084)
XLA Ops:
  1.9 15.9 %shard_map.77 = (f32[256]{0:T(256)S(1)}, f32[256]{0:T(256)S(1)}, f32[256]{0:T(256)S(1)}) custom-call(f32[16,256]{1,0:T(8,128)} %cur_hbm.1, f32[16,256]{1,0:T(8,128)} %next_hbm.1, f32[1,256]{1,0:T(1,128)} %bitcast.3, f32[12,16]{1,0:T(8,128)} %vol_hbm.1, s32[1]{0:T(128)S(6)} %copy.8.date_hbm), custom_call_target="tpu_custom_call" | custom-call | tf_op jit(solution)/shard_map/pallas_call | solution.py:285
  17.8 0.6 %maximum_maximum_fusion = (f32[256]{0:T(256)}, f32[256]{0:T(256)}) fusion(f32[256]{0:T(256)S(1)} %get-tuple-element.7, f32[]{:T(128)} %bitcast.2, f32[256]{0:T(256)S(1)} %get-tuple-element.6, f32[256]{0:T(256)S(1)} %get-tuple-element.5), kind=kLoop, calls=%fused_computation | loop fusion | flops 1280 | bytes 5124 | tf_op jit(solution)/shard_map/max | solution.py:316
